TPU v7x, 256 devices: a whole 4x4x8 slice. The times are simulated.
256 devices in a mesh: section: 2 (over y_hi), pb: 16 (over z, core), fsdp: 8 (over x, y_lo).
Axes of the slice: x: 4, y: 4 (y_hi: 2, y_lo: 2; y = y_hi * 2 + y_lo), z: 8, core: 2. Of those that a mesh axis runs over, the one named last changes fastest.
Arguments:
- decoder_states: bfloat16 [16, 32, 4096], P('pb', None, 'fsdp'), may hold values from -90 to 90
- norm_gain: bfloat16 [4096], P('fsdp'), may hold values from 0.099609375 to 1.8984375
- query_weight: bfloat16 [4096, 2048], P('fsdp', 'section'), may hold values from -0.046875 to 0.046875
- key_weight: bfloat16 [4096, 2048], P(('pb', 'fsdp'), 'section'), may hold values from -0.09375 to 0.09375
- value_weight: bfloat16 [4096, 2048], P(('pb', 'fsdp'), 'section'), may hold values from -0.09375 to 0.09375
- out_weight: bfloat16 [2048, 4096], P('section', 'fsdp'), may hold values from -0.5 to 0.5
- passage_states: bfloat16 [16, 4096, 4096], P('fsdp', 'pb'), may hold values from -400 to 400
- block_mask: int32 [16, 32], replicated, may hold values from 0 to 1, as said below
Outputs:
- cross_out: bfloat16 [16, 32, 4096], P('pb', None, 'fsdp')
Inputs may be any that keep to these rules, and one draw needn't show every extreme that they name: `block_mask`: every question has at least one live block.
All inputs are finite; a program needn't handle non-finite values.
Results may differ from a plain program's by a relative error of at most 0.01.
The roundings to bfloat16 on the way count: a program that leaves them out, or rounds other values in their place, can miss the bound.
Values may be sent and summed in bfloat16 or wider, within the bound.
A program may use at most 128 MiB of HBM per device.

v0:
```python
import jax
import jax.numpy as jnp
from jax import lax
from jax.sharding import PartitionSpec as P

HD = 64
BLOCK = 128
PASSAGE = 256


NEGATIVE = -1e30


def joined(value, axis, combine):
    everything = jax.tree.map(lambda part: lax.all_gather(part, axis), value)
    leading = jax.tree.map(lambda part: part[0], everything)

    def turn(k, so_far):
        return combine(so_far, jax.tree.map(lambda part: part[k], everything))

    return lax.fori_loop(1, lax.axis_size(axis), turn, leading)


def pack_order(alive_flags):
    amount = alive_flags.shape[0]
    ahead_count = jnp.cumsum(alive_flags) - alive_flags
    behind = jnp.cumsum(1 - alive_flags) - (1 - alive_flags)
    filled = jnp.sum(alive_flags)
    slot_index = jnp.where(alive_flags > 0, ahead_count, filled + behind)
    places = jnp.arange(amount, dtype=jnp.int32)
    order_index = jnp.sum(
        jnp.where(slot_index[None, :] == places[:, None], places[None, :], 0), axis=1
    )
    return (slot_index, order_index, filled)


def project(pieces, alive_flags, stacked):
    amount, piece_rows, model_width = pieces.shape
    slot_index, order_index, filled = pack_order(alive_flags)
    packed = pieces[order_index]
    per_group = min(amount, max(1, 256 // piece_rows))
    columns = stacked.shape[1]

    def compute(row_block):
        return jnp.dot(row_block, stacked, preferred_element_type=jnp.float32).astype(jnp.bfloat16)

    def skipped(row_block):
        return jnp.zeros((row_block.shape[0], columns), jnp.bfloat16)

    def advance(group_index, buffer):
        first_piece = group_index * per_group
        row_block = lax.dynamic_slice_in_dim(packed, first_piece, per_group, 0).reshape(
            per_group * piece_rows, model_width
        )
        result = lax.cond(first_piece < filled, compute, skipped, row_block)
        return lax.dynamic_update_slice_in_dim(
            buffer, result.reshape(per_group, piece_rows, columns), first_piece, 0
        )

    empty_buffer = jnp.zeros((amount, piece_rows, columns), jnp.bfloat16)
    buffer = lax.fori_loop(0, amount // per_group, advance, empty_buffer)
    return (buffer, slot_index, filled)


def attend(query, keyval, live_rows):
    row_total, doubled = keyval.shape
    half_width = doubled // 2
    head_count = half_width // HD
    answer_len = query.shape[0]
    keys_part = keyval[:, :half_width].reshape(row_total, head_count, HD)
    values_part = keyval[:, half_width:].reshape(row_total, head_count, HD)
    queries = query.reshape(answer_len, head_count, HD)
    scores = jnp.einsum("ahd,rhd->ahr", queries, keys_part, preferred_element_type=jnp.float32)
    shown = live_rows[None, None, :]
    scores = jnp.where(shown, scores, NEGATIVE)
    peak = jnp.max(scores, axis=2)
    raw_weights = jnp.where(shown, jnp.exp(scores - peak[:, :, None]), 0.0)
    totals = jnp.sum(raw_weights, axis=2)
    numerator = jnp.einsum(
        "ahr,rhd->ahd",
        raw_weights.astype(jnp.bfloat16),
        values_part,
        preferred_element_type=jnp.float32,
    )
    return (peak, totals, numerator)


def combine_parts(first, second):
    peak_one, totals_one, numer_one = first
    peak_two, totals_two, numer_two = second
    peak = jnp.maximum(peak_one, peak_two)
    factor_one = jnp.exp(peak_one - peak)
    factor_two = jnp.exp(peak_two - peak)
    totals = totals_one * factor_one + totals_two * factor_two
    numerator = numer_one * factor_one[:, :, None] + numer_two * factor_two[:, :, None]
    return (peak, totals, numerator)


def shards(
    decoder_states,
    norm_gain,
    query_weight,
    key_weight,
    value_weight,
    out_weight,
    passage_states,
    block_mask,
):
    pb_count = lax.axis_size("pb")
    fsdp_count = lax.axis_size("fsdp")
    pb_index = lax.axis_index("pb")
    fsdp_index = lax.axis_index("fsdp")
    local_questions, local_rows, model_width = passage_states.shape
    block_total = block_mask.shape[1]
    passages_here = local_rows // PASSAGE
    piece_rows = PASSAGE // fsdp_count
    block_ids = jnp.arange(block_total, dtype=jnp.int32)
    own_mask = lax.dynamic_slice_in_dim(block_mask, pb_index, 1, 0)[0]
    passage_ids = jnp.arange(pb_count * passages_here, dtype=jnp.int32)
    piece_block = (passage_ids * PASSAGE + fsdp_index * piece_rows) // BLOCK
    decoder_live = jnp.sum(
        jnp.where(piece_block[:, None] == block_ids[None, :], own_mask[None, :], 0), axis=1
    )
    stacked_local = jnp.concatenate([key_weight, value_weight], axis=1)
    stacked = lax.all_gather(stacked_local, ("pb", "fsdp"), axis=0, tiled=True)
    own_states = decoder_states[0]
    states_wide = own_states.astype(jnp.float32)
    square_part = jnp.sum(states_wide * states_wide, axis=1)
    scaled = (states_wide * norm_gain.astype(jnp.float32)[None, :]).astype(jnp.bfloat16)
    query_part = jnp.dot(scaled, query_weight, preferred_element_type=jnp.float32)
    square_sum, query_raw = lax.psum((square_part, query_part), "fsdp")
    query = (query_raw * lax.rsqrt(square_sum / model_width + 1e-06)[:, None]).astype(jnp.bfloat16)
    shaped = passage_states.reshape(
        local_questions, passages_here, fsdp_count, piece_rows, model_width
    )
    by_piece = lax.all_to_all(shaped, "fsdp", split_axis=2, concat_axis=0, tiled=True)
    by_question = lax.all_to_all(by_piece, "pb", split_axis=0, concat_axis=1, tiled=True)
    pieces = by_question.reshape(pb_count * passages_here, piece_rows, model_width)
    projected, slot_index, filled = project(pieces, decoder_live, stacked)
    keyval = projected.reshape(pb_count * passages_here * piece_rows, projected.shape[2])
    live_rows = jnp.repeat(passage_ids < filled, piece_rows)
    peak, totals, numerator = attend(query, keyval, live_rows)
    peak, totals, numerator = joined((peak, totals, numerator), "fsdp", combine_parts)
    attention = (
        (numerator / totals[:, :, None])
        .astype(jnp.bfloat16)
        .reshape(query.shape[0], query.shape[1])
    )
    partial_out = jnp.dot(attention, out_weight, preferred_element_type=jnp.float32)
    summed_out = lax.psum(partial_out.astype(jnp.bfloat16), "section")
    return summed_out[None]


def solution(mesh):
    placed = (
        P("pb", None, "fsdp"),
        P("fsdp"),
        P("fsdp", "section"),
        P(("pb", "fsdp"), "section"),
        P(("pb", "fsdp"), "section"),
        P("section", "fsdp"),
        P("fsdp", "pb", None),
        P(),
    )
    return jax.shard_map(
        shards, mesh=mesh, in_specs=placed, out_specs=P("pb", None, "fsdp"), check_vma=False
    )
```

profile of v0, /device:TPU:1, one launch (start us, length us, event | category | flops | bytes accessed | tf_op | source)
XLA Modules:
  0.0 605.4 jit_solution(16918323972855639439)
XLA Ops:
  7.4 0.8 convert_element_type.37
  8.1 0.5 copy-done
  8.6 1.7 fusion.15
  10.4 1.5 pad_maximum_fusion
  11.9 2.5 copy.54
  14.4 58.9 %all_to_all.27 = bf16[2,1,8,32,4096]{4,3,0,1,2:T(8,128)(2,1)} all-to-all(bf16[2,1,8,32,4096]{4,3,0,1,2:T(8,128)(2,1)S(1)} %copy.54), channel_id=1, replica_groups=mesh['section'=2,'pb'=16,'fsdp'=8] {'fsdp'}, dimensions={2} | all-to-all | bytes 8388608 | tf_op jit(solution)/shard_map/all_to_all | solution.py:136
  73.3 11.3 %all-to-all-start.1 = ((bf16[16,1,1,32,4096]{4,3,2,1,0:T(8,128)(2,1)}), bf16[16,1,1,32,4096]{4,3,2,1,0:T(8,128)(2,1)}, u32[]{:S(2)}, u32[]{:S(2)}) async-start(bf16[16,1,1,32,4096]{4,3,2,1,0:T(8,128)(2,1)} %bitcast.72), calls=%async_computation.1 | async-start | bytes 8388608 | tf_op jit(solution)/shard_map/all_to_all | solution.py:137
  84.7 0.7 dynamic-slice_bitcast_fusion
  85.4 0.7 select_reduce_fusion
  86.2 0.1 reduce.2
  86.5 0.1 reduce.1
  86.6 0.6 iota_compare_fusion.2
  87.2 0.1 broadcast_in_dim.77
  87.3 0.1 fusion.14
  87.5 16.6 %psum.22 = f32[32]{0:T(128)S(1)} all-reduce(f32[32]{0:T(128)S(1)} %fusion.14), channel_id=1, replica_groups=mesh['section'=2,'pb'=16,'fsdp'=8] {'fsdp'}, use_global_device_ids=true, to_apply=%region_11.12 | all-reduce | flops 32 | bytes 256 | tf_op jit(solution)/shard_map/psum | solution.py:131
  104.0 0.6 compare_select_fusion.1
  104.6 0.1 select_reduce_fusion.2
  104.8 5.6 all-reduce.2.cloned.1.call-done
  110.4 1.0 multiply_convert_fusion
  111.4 0.1 reshape.158
  111.5 77.8 %all-to-all-done.1 = bf16[16,1,1,32,4096]{4,3,2,1,0:T(8,128)(2,1)} async-done(((bf16[16,1,1,32,4096]{4,3,2,1,0:T(8,128)(2,1)}), bf16[16,1,1,32,4096]{4,3,2,1,0:T(8,128)(2,1)}, u32[]{:S(2)}, u32[]{:S(2)}) %all-to-all-start.1) | async-done | bytes 4194336 | tf_op jit(solution)/shard_map/all_to_all | solution.py:137
  189.3 4.9 gather_fusion
  194.2 275.4 %all-gather.8.cloned.1.call-done = bf16[4096,2048]{1,0:T(8,128)(2,1)} async-done(((bf16[32,2048]{1,0:T(8,128)(2,1)}), bf16[4096,2048]{1,0:T(8,128)(2,1)}) %all-gather.8.cloned.1.call-update) | async-done | bytes 16777232 | tf_op jit(solution)/shard_map/all_gather | solution.py:125
  469.7 1.6 broadcast_in_dim.79
  471.2 23.5 %while.32 = (s32[]{:T(128)}, bf16[16,32,2048]{2,1,0:T(8,128)(2,1)}, s32[]{:T(128)}, bf16[16,32,4096]{2,1,0:T(8,128)(2,1)}, bf16[4096,2048]{1,0:T(8,128)(2,1)}, /*index=5*/s32[]{:T(128)}, s32[]{:T(128)}, s32[]{:T(128)}, s32[]{:T(128)}) while((s32[]{:T(128)}, bf16[16,32,2048]{2,1,0:T(8,128)(2,1)}, s32[]{:T(128)}, ...), condition=%wide.region_8.9_spmd, body=%wide.region_5.8_spmd.sunk | while | flops 4295491584 | bytes 26215100 | solution.py:61
  471.8 10.1 %conditional.2 = (bf16[8,32,2048]{2,1,0:T(8,128)(2,1)S(1)}) conditional(s32[]{:T(128)} %convert_element_type.55, () %tuple.82, (bf16[16,32,4096]{2,1,0:T(8,128)(2,1)}, s32[]{:T(128)}, bf16[4096,2048]{1,0:T(8,128)(2,1)}) %tuple.83), branch_computations={%region_6.6_spmd, %region_7.7_spmd} | conditional | flops 4295491584 | bytes 24117260 | solution.py:55
  471.8 1.8 constant_dynamic-slice_fusion
  473.6 8.3 %convolution_convert_fusion = bf16[256,2048]{1,0:T(8,128)(2,1)S(1)} fusion(bf16[256,4096]{1,0:T(8,128)(2,1)S(1)} %bitcast.71, bf16[4096,2048]{1,0:T(8,128)(2,1)} %get-tuple-element.284), kind=kOutput, calls=%fused_computation.1 | convolution fusion | flops 4295491584 | bytes 19922944 | tf_op jit(solution)/shard_map/while/body/eval_jaxpr/cond/branch_1_fun/dot_general | solution.py:45
  481.9 1.0 constant_dynamic-update-slice_fusion.2
  483.6 10.1 %conditional.2 = (bf16[8,32,2048]{2,1,0:T(8,128)(2,1)S(1)}) conditional(s32[]{:T(128)} %convert_element_type.55, () %tuple.82, (bf16[16,32,4096]{2,1,0:T(8,128)(2,1)}, s32[]{:T(128)}, bf16[4096,2048]{1,0:T(8,128)(2,1)}) %tuple.83), branch_computations={%region_6.6_spmd, %region_7.7_spmd} | conditional | flops 4295491584 | bytes 24117260 | solution.py:55
  483.6 1.8 constant_dynamic-slice_fusion
  485.4 8.3 %convolution_convert_fusion = bf16[256,2048]{1,0:T(8,128)(2,1)S(1)} fusion(bf16[256,4096]{1,0:T(8,128)(2,1)S(1)} %bitcast.71, bf16[4096,2048]{1,0:T(8,128)(2,1)} %get-tuple-element.284), kind=kOutput, calls=%fused_computation.1 | convolution fusion | flops 4295491584 | bytes 19922944 | tf_op jit(solution)/shard_map/while/body/eval_jaxpr/cond/branch_1_fun/dot_general | solution.py:45
  493.7 1.1 constant_dynamic-update-slice_fusion.2
  494.8 2.7 fusion.22
  497.5 1.5 copy.65
  499.0 1.3 copy.66
  500.3 0.4 fusion.23
  500.7 0.9 copy-done.1
  501.5 1.2 convolution_bitcast_fusion
  502.8 0.3 fusion.7
  503.1 22.0 %all-gather.4 = f32[8,32,16]{1,2,0:T(8,128)S(1)} all-gather(f32[1,32,16]{1,2,0:T(8,128)S(1)} %bitcast.79), channel_id=3, replica_groups=mesh['section'=2,'pb'=16,'fsdp'=8] {'fsdp'}, dimensions={0}, use_global_device_ids=true | all-gather | bytes 18432 | tf_op jit(solution)/shard_map/all_gather | solution.py:15
  525.1 22.9 %all-gather.3 = f32[8,32,16]{1,2,0:T(8,128)S(1)} all-gather(f32[1,32,16]{1,2,0:T(8,128)S(1)} %bitcast.78), channel_id=2, replica_groups=mesh['section'=2,'pb'=16,'fsdp'=8] {'fsdp'}, dimensions={0}, use_global_device_ids=true | all-gather | bytes 18432 | tf_op jit(solution)/shard_map/all_gather | solution.py:15
  548.1 26.8 %all-gather.10.cloned.1.call-done = f32[256,16,64]{2,0,1:T(8,128)} async-done(((f32[32,16,64]{2,0,1:T(8,128)}), f32[256,16,64]{2,0,1:T(8,128)}) %all-gather.10.cloned.1.call-update) | async-done | bytes 1048592 | tf_op jit(solution)/shard_map/all_gather | solution.py:15
  574.9 1.0 slice.31
  575.8 0.2 copy.61
  576.0 10.5 %while.33 = (s32[]{:T(128)}, f32[32,16]{0,1:T(8,128)S(1)}, f32[32,16]{0,1:T(8,128)S(1)}, f32[32,16,64]{2,1,0:T(8,128)S(1)}, f32[8,32,16]{1,2,0:T(8,128)S(1)}, /*...) while((s32[]{:T(128)}, f32[32,16]{0,1:T(8,128)S(1)}, ...), condition=%wide.region_15.16_spmd, body=%wide.region_14.15_spmd.sunk | while | flops 101381 | bytes 684183 | solution.py:21
  576.2 1.1 constant_dynamic-slice_fusion.3
  577.3 0.3 fusion.34
  577.8 1.0 constant_dynamic-slice_fusion.3
  578.8 0.3 fusion.34
  579.3 1.0 constant_dynamic-slice_fusion.3
  580.3 0.3 fusion.34
  580.8 1.0 constant_dynamic-slice_fusion.3
  581.7 0.3 fusion.34
  582.2 1.0 constant_dynamic-slice_fusion.3
  583.2 0.3 fusion.34
  583.7 1.0 constant_dynamic-slice_fusion.3
  584.7 0.3 fusion.34
  585.2 1.0 constant_dynamic-slice_fusion.3
  586.2 0.3 fusion.34
  586.6 0.1 divide_convert_fusion
  586.7 0.1 reshape.160
  586.9 0.3 fusion.5
  587.1 10.8 %psum.23 = bf16[1,32,512]{2,1,0:T(8,128)(2,1)} all-reduce(bf16[1,32,512]{2,1,0:T(8,128)(2,1)S(1)} %fusion.5), channel_id=1, replica_groups=mesh['section'=2,'pb'=16,'fsdp'=8] {'section'}, use_global_device_ids=true, to_apply=%region_16.17 | all-reduce | flops 16384 | bytes 65536 | tf_op jit(solution)/shard_map/psum | solution.py:150
  (46 shorter events, 1.7 us)
Async XLA Ops:
  7.4 1.2 copy-start
  7.4 103.0 %all-reduce.2.cloned.1.call-start = ((), (), s32[]{:S(2)}) async-start(), calls=%async_computation.3 | async-start | bytes 262144 | tf_op jit(solution)/shard_map/psum | solution.py:131
  10.3 459.3 %all-gather.8.cloned.1.call-start = ((), (), s32[]{:S(2)}) async-start(), calls=%async_computation.2 | async-start | bytes 16908288 | tf_op jit(solution)/shard_map/all_gather | solution.py:125
  73.3 14.0 %copy-start.3 = (bf16[1,32,512]{2,1,0:T(8,128)(2,1)S(1)}, bf16[1,32,512]{2,1,0:T(8,128)(2,1)}, u32[]{:S(2)}) copy-start(bf16[1,32,512]{2,1,0:T(8,128)(2,1)} %param.14) | copy-start | bytes 98308
  73.3 116.0 %all-to-all-start.1 = ((bf16[16,1,1,32,4096]{4,3,2,1,0:T(8,128)(2,1)}), bf16[16,1,1,32,4096]{4,3,2,1,0:T(8,128)(2,1)}, u32[]{:S(2)}, u32[]{:S(2)}) async-start(bf16[16,1,1,32,4096]{4,3,2,1,0:T(8,128)(2,1)} %bitcast.72), calls=%async_computation.1 | async-start | bytes 8388608 | tf_op jit(solution)/shard_map/all_to_all | solution.py:137
  84.7 490.2 %all-gather.10.cloned.1.call-start = ((), (), s32[]{:S(2)}) async-start(), calls=%async_computation.4 | async-start | bytes 2359296 | tf_op jit(solution)/shard_map/all_gather | solution.py:15
  500.3 1.2 copy-start.1
  576.0 10.8 %copy-start.2 = (bf16[1024,512]{1,0:T(8,128)(2,1)S(1)}, bf16[1024,512]{1,0:T(8,128)(2,1)}, u32[]{:S(2)}) copy-start(bf16[1024,512]{1,0:T(8,128)(2,1)} %param.19) | copy-start | bytes 3145732
Sparse Core Ops, SparseCore 0:
  10.8 99.5 all-reduce.1
  502.9 71.9 all-gather.9
Sparse Core Ops, SparseCore 1:
  12.6 457.0 all-gather.7
where the time goes:
time: 608 us; the launch traced here: 605 us
  waiting for transfers between devices  386 us (63%)
  blocking collectives  131 us (22%)
  local copies, waits for them, and re-layouts  32.1 us (5%)
  matrix products  20.1 us (3%)
  between operations  15 us (2%)
  starting transfers between devices  11.4 us (2%)
  other arithmetic  8.4 us (1%)
    all_gather x1, waiting for transfers between devices, shards(): stacked = lax.all_gather(stacked_local, ('pb', 'fsdp'), axis=0, tiled=True)  275 us
    all_to_all x1, waiting for transfers between devices, shards(): lax.all_to_all(by_piece, 'pb', split_axis=0, concat_axis=1, tiled=True)  77.8 us
    all_to_all x1, blocking collectives, shards(): lax.all_to_all(shaped, 'fsdp', split_axis=2, concat_axis=0, tiled=True)  58.9 us
    all_gather x2, blocking collectives, joined(): everything = jax.tree.map(lambda part: lax.all_gather(part, axis), value)  44.9 us
    all_gather x1, waiting for transfers between devices, joined(): everything = jax.tree.map(lambda part: lax.all_gather(part, axis), value)  26.8 us
    psum x1, blocking collectives, shards(): square_sum, query_raw = lax.psum((square_part, query_part), 'fsdp')  16.6 us
    dot_general x2, matrix products, compute(): jnp.dot(row_block, stacked, preferred_element_type=jnp.float32)  16.6 us
  transfers between devices with their start and end apart: 4, of which 4 were waited for; matrix products, arithmetic and copies ran while one was open for 2% of the time, Pallas kernels for 0%

commit v1 on v0

v1 whole, which is shorter than its diff:
```python
import jax
import jax.numpy as jnp
from jax import lax
from jax.experimental import pallas as pl
from jax.experimental.pallas import tpu as pltpu
from jax.sharding import PartitionSpec as P

HD = 64
BLOCK = 128
NEGATIVE = -1e30
MESH = pl.DeviceIdType.MESH
NZ = 8
NX = 4
SPLIT = 384
F32 = jnp.float32
BF16 = jnp.bfloat16


def kernel(
    mask_ref, ds_ref, gain_ref, qw_ref, kw_ref, vw_ref, ow_ref, pass_ref, out_ref,
    xs, ws, acc, ow, ds, gain, qw, qpart, qrecv, qsend, qbuf, part, recv, asend, att,
    loc, pair_s, pair_r, y_s, y_r, ax_s, ax_r, az_s, az_r, bz_s, bz_r, bx_s, bx_r,
    q2_s, q2_r, q3_s, q3_r, ow_s, ow_r, t1_s, t1_r, t2_s, t2_r,
):
    s = lax.axis_index("section")
    p = lax.axis_index("pb")
    f = lax.axis_index("fsdp")
    z, c = p // 2, lax.rem(p, 2)
    x, y = f // 2, lax.rem(f, 2)

    def zat(k):
        return lax.rem(z + k + NZ, NZ)

    def xat(k):
        return lax.rem(x + k + NX, NX)

    def dev(s_, p_, f_):
        return {"section": s_, "pb": p_, "fsdp": f_}

    partner = dev(s, z * 2 + 1 - c, f)
    ynear = dev(s, p, x * 2 + 1 - y)
    xdev = {k: dev(s, p, xat(k) * 2 + y) for k in (1, -1)}
    zdev = {k: dev(s, zat(k) * 2 + c, f) for k in (1, -1)}
    other_section = dev(1 - s, p, f)

    def rcopy(src, dst, ssem, rsem, to):
        return pltpu.make_async_remote_copy(
            src_ref=src, dst_ref=dst, send_sem=ssem, recv_sem=rsem, device_id=to, device_id_type=MESH
        )

    def half(ref, h):
        return ref.at[:, pl.ds(pl.multiple_of(h * 512, 512), 512)]

    locals_ = [
        pltpu.make_async_copy(ds_ref, ds, loc.at[0]),
        pltpu.make_async_copy(gain_ref, gain, loc.at[1]),
        pltpu.make_async_copy(qw_ref, qw, loc.at[2]),
        pltpu.make_async_copy(half(kw_ref, c), ws.at[z, c, f, :, pl.ds(0, 512)], loc.at[3]),
        pltpu.make_async_copy(half(vw_ref, c), ws.at[z, c, f, :, pl.ds(512, 512)], loc.at[4]),
        pltpu.make_async_copy(pass_ref, xs.at[c], loc.at[5]),
        pltpu.make_async_copy(ow_ref, ow.at[s], loc.at[6]),
    ]
    for copy in locals_:
        copy.start()

    barrier = pltpu.get_barrier_semaphore()

    def greet(to):
        pl.semaphore_signal(barrier, inc=1, device_id=to, device_id_type=MESH)

    def greet_maybe(is_self, to):
        @pl.when(jnp.logical_not(is_self))
        def _():
            greet(to)

    def q3_target(k):
        return zat(k), f // 4, z

    def t2_target(ds_, k):
        return lax.rem(s + ds_, 2), f * 2 + z // 4, lax.rem(f + k, 8)

    for to in (partner, ynear, xdev[1], xdev[-1], zdev[1], zdev[-1], other_section):
        greet(to)
    for k in range(1, 8):
        greet(dev(s, p, lax.rem(f + k, 8)))
        greet(dev(s, zat(k) * 2 + c, f))
    diag = z == f
    for k in range(8):
        zt, ct, ft = q3_target(k)
        to = dev(s, zt * 2 + ct, ft)
        if k == 0:
            greet_maybe(diag & (ct == c), to)
        else:
            greet(to)
    for ds_ in range(2):
        for k in range(8):
            st, pt, ft = t2_target(ds_, k)
            to = dev(st, pt, ft)
            if ds_ == 0 and k == 0:
                greet_maybe(pt == p, to)
            else:
                greet(to)
    selves = jnp.where(diag & (f // 4 == c), 1, 0) + jnp.where(f * 2 + z // 4 == p, 1, 0)
    pl.semaphore_wait(barrier, 7 + 14 + 8 + 16 - selves)

    sends = []

    def go(copy):
        copy.start()
        sends.append(copy)

    def pair_copy(i):
        w_ref = (kw_ref, vw_ref)[i]
        return rcopy(
            half(w_ref, 1 - c), ws.at[z, c, f, :, pl.ds(512 * i, 512)], pair_s.at[i], pair_r.at[i], partner
        )

    go(pair_copy(0))
    go(pair_copy(1))
    go(rcopy(pass_ref, xs.at[c], pair_s.at[2], pair_r.at[2], partner))

    def land(dst, rsem):
        rcopy(dst, dst, loc.at[7], rsem, partner).wait_recv()

    def plane(i):
        if i == 0:
            return z
        if i == NZ - 1:
            return zat(NZ // 2)
        return zat(-((i + 1) // 2)) if i % 2 else zat(i // 2)

    def piece_a(zz, xx):
        return ws.at[zz, :, pl.ds(xx * 2, 2), :, pl.ds(0, SPLIT)]

    def piece_b(zz, xx):
        return ws.at[zz, :, pl.ds(xx * 2, 2), :, pl.ds(SPLIT, 1024 - SPLIT)]

    def piece_bh(zz, xx, h):
        return ws.at[zz, h, pl.ds(xx * 2, 2), :, pl.ds(SPLIT, 1024 - SPLIT)]

    def onward(i, parity):
        if i == NZ - 1:
            return None
        k = (i + 1) // 2
        way = 1 if i % 2 else -1
        if k + 1 < NZ // 2:
            return (i + 2, way)
        if (parity == 0) == (way == 1):
            return (NZ - 1, way)
        return None

    def z_sends(ref, i, col, ssem, rsem):
        nexts = [(1, 1), (2, -1)] if i == 0 else [onward(i, col % 2)]
        for step in nexts:
            if step is not None:
                slot, way = step
                go(rcopy(ref, ref, ssem.at[slot - 1, col], rsem.at[slot - 1, col], zdev[way]))

    xorder = (0, -1, 1, 2)

    def b_z(i):
        for h in range(2):
            ref = piece_bh(plane(i), x, h)
            if i > 0:
                land(ref, bz_r.at[i - 1, h])
            z_sends(ref, i, h, bz_s, bz_r)
        ref = piece_b(plane(i), x)
        go(rcopy(ref, ref, bx_s.at[i, 0], bx_r.at[i, 0], xdev[1]))
        go(rcopy(ref, ref, bx_s.at[i, 1], bx_r.at[i, 1], xdev[-1]))

    def a_z(i):
        for j in range(4):
            ref = piece_a(plane(i), xat(xorder[j]))
            if i > 0:
                land(ref, az_r.at[i - 1, j])
            elif j > 0:
                land(ref, ax_r.at[j - 1])
                if j == 1:
                    go(rcopy(ref, ref, ax_s.at[2], ax_r.at[2], xdev[1]))
            z_sends(ref, i, j, az_s, az_r)

    def b_x1(i):
        left, right = piece_b(plane(i), xat(-1)), piece_b(plane(i), xat(1))
        land(left, bx_r.at[i, 0])
        if i % 2 == 0:
            go(rcopy(left, left, bx_s.at[i, 2], bx_r.at[i, 2], xdev[1]))
        land(right, bx_r.at[i, 1])
        if i % 2 == 1:
            go(rcopy(right, right, bx_s.at[i, 2], bx_r.at[i, 2], xdev[-1]))

    def b_x2(i):
        land(piece_b(plane(i), xat(2)), bx_r.at[i, 2])

    def project(i):
        zz = plane(i)
        cols = pl.ds(pl.multiple_of(zz * 512, 512), 512)

        def tile(t, carry):
            rows = xs[t // 2, lax.rem(t, 2), :, cols]
            for n in range(4):
                w = ws[zz, :, :, :, n * 256 : (n + 1) * 256].reshape(512, 256)
                term = jnp.dot(rows, w, preferred_element_type=F32)
                at = (t, slice(None), slice(n * 256, (n + 1) * 256))
                if i == 0:
                    acc[at] = term
                else:
                    acc[at] += term
            return carry

        lax.fori_loop(0, 4, tile, 0)

    def query_start():
        for copy in locals_[:3]:
            copy.wait()
        wide = ds[...].astype(F32)
        squares = jnp.broadcast_to(jnp.sum(wide * wide, axis=1, keepdims=True), (32, 128))
        scaled = (wide * gain[...].astype(F32)).astype(BF16)
        total = jnp.dot(scaled, qw[...], preferred_element_type=F32)
        for b in range(8):
            qpart[b, :, 0:128] = total[:, b * 128 : (b + 1) * 128]
            qpart[b, :, 128:256] = squares

    def query_reduce():
        for k in range(1, 8):
            to = lax.rem(f + k, 8)
            go(rcopy(qpart.at[to], qrecv.at[k - 1], q2_s.at[k - 1], q2_r.at[k - 1], dev(s, p, to)))

    def query_send():
        total = qpart[f]
        for k in range(7):
            land(qrecv.at[k], q2_r.at[k])
            total = total + qrecv[k]
        scale = lax.rsqrt(total[:, 128:256] / 4096.0 + 1e-06)
        qsend[...] = (total[:, 0:128] * scale).astype(BF16)
        block = lax.rem(f, 4)
        for k in range(8):
            zt, ct, ft = q3_target(k)
            copy = rcopy(
                qsend, qbuf.at[c, block], q3_s.at[k], q3_r.at[c * 4 + block], dev(s, zt * 2 + ct, ft)
            )
            if k == 0:
                own = diag & (ct == c)

                @pl.when(own)
                def _():
                    qbuf[c, block] = qsend[...]

                @pl.when(jnp.logical_not(own))
                def _():
                    copy.start()

            else:
                go(copy)

    def query_wait():
        for cs in range(2):
            for b in range(4):
                own = diag & (f // 4 == c) & (cs == c) & (b == lax.rem(f, 4))

                @pl.when(jnp.logical_not(own))
                def _():
                    land(qbuf.at[cs, b], q3_r.at[cs * 4 + b])

        zt, ct, ft = q3_target(0)

        @pl.when(jnp.logical_not(diag & (ct == c)))
        def _():
            rcopy(qsend, qbuf.at[0, 0], q3_s.at[0], q3_r.at[0], partner).wait_send()

    def attend():
        head_of = lax.broadcasted_iota(jnp.int32, (32, 512), 1) // HD
        lane = lax.broadcasted_iota(jnp.int32, (32, 128), 1)
        block_of = lax.broadcasted_iota(jnp.int32, (256, 512), 1) // BLOCK
        for q in range(2):
            query = jnp.concatenate([qbuf[q, b] for b in range(4)], axis=1).astype(F32)
            spread = jnp.concatenate(
                [jnp.where(head_of == h, query, 0.0).astype(BF16) for h in range(8)], axis=0
            )
            keys = jnp.concatenate([acc[q, :, 0:512], acc[2 + q, :, 0:512]], axis=0).astype(BF16)
            values = jnp.concatenate([acc[q, :, 512:1024], acc[2 + q, :, 512:1024]], axis=0).astype(BF16)
            scores = lax.dot_general(spread, keys, (((1,), (1,)), ((), ())), preferred_element_type=F32)
            flags = jnp.zeros((256, 512), jnp.int32)
            for b in range(4):
                flags = jnp.where(block_of == b, mask_ref[f * 2 + q, z * 4 + b], flags)
            shown = flags > 0
            scores = jnp.where(shown, scores, NEGATIVE)
            peak = jnp.max(scores, axis=1, keepdims=True)
            raw = jnp.where(shown, jnp.exp(scores - peak), 0.0)
            totals = jnp.sum(raw, axis=1, keepdims=True)
            wide = jnp.dot(raw.astype(BF16), values, preferred_element_type=F32)
            numer = jnp.zeros((32, 512), F32)
            stats = jnp.zeros((32, 128), F32)
            for h in range(8):
                rows = slice(h * 32, (h + 1) * 32)
                numer = jnp.where(head_of == h, wide[rows], numer)
                stats = jnp.where(lane == h, peak[rows], stats)
                stats = jnp.where(lane == h + 64, totals[rows], stats)
            for ah in range(2):
                rows = slice(ah * 16, (ah + 1) * 16)
                for ch in range(2):
                    rank = (q * 2 + ah) * 2 + ch
                    part[rank, :, 0:256] = numer[rows, ch * 256 : (ch + 1) * 256]
                    part[rank, :, 256:384] = stats[rows]

    def combine_send():
        for k in range(1, 8):
            zt = zat(k)
            go(rcopy(part.at[zt], recv.at[k - 1], t1_s.at[k - 1], t1_r.at[k - 1], dev(s, zt * 2 + c, f)))

    def combine():
        pieces = [part[z]]
        for k in range(7):
            land(recv.at[k], t1_r.at[k])
            pieces.append(recv[k])
        top = pieces[0][:, 256:384]
        for piece in pieces[1:]:
            top = jnp.maximum(top, piece[:, 256:384])
        col_head = lax.broadcasted_iota(jnp.int32, (16, 256), 1) // HD
        first = lax.rem(z, 2) == 0

        def widen(stat, base):
            low = jnp.zeros((16, 256), F32)
            for h in range(4):
                one = jnp.where(first, stat[:, base + h : base + h + 1], stat[:, base + h + 4 : base + h + 5])
                low = jnp.where(col_head == h, one, low)
            return low

        top_wide = widen(top, 0)
        numer = jnp.zeros((16, 256), F32)
        total = jnp.zeros((16, 256), F32)
        for piece in pieces:
            stat = piece[:, 256:384]
            factor = jnp.exp(widen(stat, 0) - top_wide)
            numer = numer + piece[:, 0:256] * factor
            total = total + widen(stat, 64) * factor
        asend[...] = (numer / total).astype(BF16)

    def spot():
        return s, c, lax.rem(z, 2), lax.rem(z // 2, 2)

    def scatter():
        a, b, d, e = spot()
        sem = t2_r.at[((a * 2 + b) * 2 + d) * 2 + e]
        for ds_ in range(2):
            for k in range(8):
                st, pt, ft = t2_target(ds_, k)
                copy = rcopy(asend, att.at[a, b, d, e], t2_s.at[ds_ * 8 + k], sem, dev(st, pt, ft))
                if ds_ == 0 and k == 0:
                    own = pt == p

                    @pl.when(own)
                    def _():
                        att[a, b, d, e] = asend[...]

                    @pl.when(jnp.logical_not(own))
                    def _():
                        copy.start()

                else:
                    go(copy)

    def finish():
        locals_[6].wait()
        land(ow.at[1 - s], ow_r.at[0])
        a, b, d, e = spot()
        own_code = ((a * 2 + b) * 2 + d) * 2 + e
        st, pt, ft = t2_target(0, 0)
        own = pt == p
        total = jnp.zeros((32, 512), F32)
        for si in range(2):
            for ci in range(2):
                for ch in range(2):
                    halves = []
                    for ah in range(2):
                        code = ((si * 2 + ci) * 2 + ch) * 2 + ah

                        @pl.when(jnp.logical_not(own & (own_code == code)))
                        def _():
                            land(att.at[si, ci, ch, ah], t2_r.at[code])

                        halves.append(att[si, ci, ch, ah])
                    rows = jnp.concatenate(halves, axis=0)
                    at = ci * 512 + ch * 256
                    total = total + jnp.dot(rows, ow[si, at : at + 256, :], preferred_element_type=F32)
        out_ref[...] = total.astype(BF16)

        @pl.when(jnp.logical_not(own))
        def _():
            rcopy(asend, att.at[0, 0, 0, 0], t2_s.at[0], t2_r.at[0], partner).wait_send()

    query_start()
    locals_[3].wait()
    locals_[4].wait()
    land(ws.at[z, 1 - c, f, :, pl.ds(0, 512)], pair_r.at[0])
    land(ws.at[z, 1 - c, f, :, pl.ds(512, 512)], pair_r.at[1])
    mine = ws.at[z, :, f]
    go(rcopy(mine, mine, y_s.at[0], y_r.at[0], ynear))
    land(ws.at[z, :, x * 2 + 1 - y], y_r.at[0])
    own_a = piece_a(z, x)
    go(rcopy(own_a, own_a, ax_s.at[0], ax_r.at[0], xdev[1]))
    go(rcopy(own_a, own_a, ax_s.at[1], ax_r.at[1], xdev[-1]))
    for t in range(NZ + 2):
        if t < NZ:
            b_z(t)
            a_z(t)
        if 1 <= t <= NZ:
            b_x1(t - 1)
        if t == 0:
            query_reduce()
        if t == 1:
            query_send()
        if t == 2:
            locals_[5].wait()
            land(xs.at[1 - c], pair_r.at[2])
            go(rcopy(ow_ref, ow.at[s], ow_s.at[0], ow_r.at[0], other_section))
        if t >= 2:
            b_x2(t - 2)
            project(t - 2)
    query_wait()
    attend()
    combine_send()
    combine()
    scatter()
    finish()
    for copy in sends:
        copy.wait_send()


def shards(
    decoder_states, norm_gain, query_weight, key_weight, value_weight, out_weight, passage_states, block_mask
):
    anywhere = pl.BlockSpec(memory_space=pl.ANY)
    dma = pltpu.SemaphoreType.DMA
    out = pl.pallas_call(
        kernel,
        out_shape=jax.ShapeDtypeStruct((32, 512), BF16),
        in_specs=[pl.BlockSpec(memory_space=pltpu.SMEM)] + [anywhere] * 7,
        out_specs=pl.BlockSpec(memory_space=pltpu.VMEM),
        scratch_shapes=[
            pltpu.VMEM((2, 2, 256, 4096), BF16),
            pltpu.VMEM((NZ, 2, 8, 32, 1024), BF16),
            pltpu.VMEM((4, 256, 1024), F32),
            pltpu.VMEM((2, 1024, 512), BF16),
            pltpu.VMEM((32, 512), BF16),
            pltpu.VMEM((1, 512), BF16),
            pltpu.VMEM((512, 1024), BF16),
            pltpu.VMEM((8, 32, 256), F32),
            pltpu.VMEM((7, 32, 256), F32),
            pltpu.VMEM((32, 128), BF16),
            pltpu.VMEM((2, 4, 32, 128), BF16),
            pltpu.VMEM((8, 16, 384), F32),
            pltpu.VMEM((7, 16, 384), F32),
            pltpu.VMEM((16, 256), BF16),
            pltpu.VMEM((2, 2, 2, 2, 16, 256), BF16),
            dma((8,)),
            dma((3,)), dma((3,)),
            dma((1,)), dma((1,)),
            dma((3,)), dma((3,)),
            dma((NZ - 1, 4)), dma((NZ - 1, 4)),
            dma((NZ - 1, 2)), dma((NZ - 1, 2)),
            dma((NZ, 3)), dma((NZ, 3)),
            dma((7,)), dma((7,)),
            dma((8,)), dma((8,)),
            dma((1,)), dma((1,)),
            dma((7,)), dma((7,)),
            dma((16,)), dma((16,)),
        ],
        compiler_params=pltpu.CompilerParams(
            collective_id=0, has_side_effects=True, vmem_limit_bytes=56 * 1024 * 1024
        ),
        name="reader",
    )(
        block_mask, decoder_states[0], norm_gain[None], query_weight, key_weight, value_weight,
        out_weight, passage_states,
    )
    return out[None]


def solution(mesh):
    placed = (
        P("pb", None, "fsdp"),
        P("fsdp"),
        P("fsdp", "section"),
        P(("pb", "fsdp"), "section"),
        P(("pb", "fsdp"), "section"),
        P("section", "fsdp"),
        P("fsdp", "pb", None),
        P(),
    )
    return jax.shard_map(
        shards, mesh=mesh, in_specs=placed, out_specs=P("pb", None, "fsdp"), check_vma=False
    )
```

time: 608 us -> 101 us (0.17)
  waiting for transfers between devices: 386 us -> 0 us
  blocking collectives: 131 us -> 0 us
  Pallas kernels: 0 us -> 98 us
  local copies, waits for them, and re-layouts: 32.1 us -> 2.63 us
  matrix products: 20.1 us -> 0 us
  between operations: 15 us -> 0.01 us
  starting transfers between devices: 11.4 us -> 0 us
  other arithmetic: 8.4 us -> 0 us
    all_gather x2 -> x0, waiting for transfers between devices: 302 us -> none  [the longest x1 275 us: shards(): stacked = lax.all_gather(stacked_local, ('pb', 'fsdp'), axis=0, tiled=True)]
    pallas_call x0 -> x1, Pallas kernels: none -> 98 us  [shards(): pl.pallas_call(kernel, out_shape=jax.ShapeDtypeStruct((32, 512), BF16), i...]
    all_to_all x1 -> x0, waiting for transfers between devices: 77.8 us -> none  [shards(): lax.all_to_all(by_piece, 'pb', split_axis=0, concat_axis=1, tiled=True)]
    all_to_all x1 -> x0, blocking collectives: 58.9 us -> none  [shards(): lax.all_to_all(shaped, 'fsdp', split_axis=2, concat_axis=0, tiled=True)]
    all_gather x2 -> x0, blocking collectives: 44.9 us -> none  [joined(): everything = jax.tree.map(lambda part: lax.all_gather(part, axis), value)]
    psum x2 -> x0, blocking collectives: 27.4 us -> none  [the longest x1 16.6 us: shards(): square_sum, query_raw = lax.psum((square_part, query_part), 'fsdp')]
    dot_general x6 -> x0, matrix products: 20.1 us -> none  [the longest x2 16.6 us: compute(): jnp.dot(row_block, stacked, preferred_element_type=jnp.float32)]
    all_to_all x1 -> x0, starting transfers between devices: 11.3 us -> none  [shards(): lax.all_to_all(by_piece, 'pb', split_axis=0, concat_axis=1, tiled=True)]
  transfers between devices with their start and end apart: 4 -> 0, of which waited for: 4 -> 0; matrix products, arithmetic and copies ran while one was open for 2% -> 0% of each run, Pallas kernels for 0% -> 0%
where the time goes in v1:
time: 101 us
  Pallas kernels  98 us (97%)
  local copies, waits for them, and re-layouts  2.63 us (3%)
    pallas_call x1, Pallas kernels, shards(): pl.pallas_call(kernel, out_shape=jax.ShapeDtypeStruct((32, 512), BF16), i...  98 us

profile of v1, /device:TPU:1, one launch (start us, length us, event | category | flops | bytes accessed | tf_op | source)
XLA Modules:
  0.0 100.6 jit_solution(12618649158998519473)
XLA Ops:
  0.0 1.3 %broadcast_in_dim.6.gain_ref = bf16[1,512]{1,0:T(2,128)(2,1)} reshape(bf16[512]{0:T(512)(128)(2,1)} %param.9) | data formatting | bytes 2048 | tf_op jit(solution)/shard_map/broadcast_in_dim | solution.py:473
  1.3 98.0 %reader.1 = bf16[32,512]{1,0:T(8,128)(2,1)} custom-call(s32[16,32]{1,0:T(8,128)} %mask_ref.1, bf16[32,512]{1,0:T(8,128)(2,1)} %bitcast.3, bf16[1,512]{1,0:T(2,128)(2,1)} %broadcast_in_dim.6.gain_ref, bf16[512,1024]{1,0:T(8,128)(2,1)} %qw_ref.1, bf16[32,1024]{1,0:T(8,128)(2,1)} %kw_ref.1, bf16[32,1024]{1,0:T(8,128)(2,1)} %vw_ref.1, bf16[1024,512]{1,0:T(8,128)(2,1)} %ow_ref.1, ...), custom_call_target="tpu_custom_call" | custom-call | tf_op jit(solution)/shard_map/reader/pallas_call | solution.py:434
  99.2 1.4 %copy.10 = bf16[1,32,512]{2,1,0:T(8,128)(2,1)} copy(bf16[1,32,512]{2,1,0:T(8,128)(2,1)} %bitcast.2) | data formatting | bytes 65536

commit v2 on v1

v2 whole, which is shorter than its diff:
```python
import jax
import jax.numpy as jnp
from jax import lax
from jax.experimental import pallas as pl
from jax.experimental.pallas import tpu as pltpu
from jax.sharding import PartitionSpec as P

HD = 64
BLOCK = 128
NEGATIVE = -1e30
MESH = pl.DeviceIdType.MESH
NZ = 8
NX = 4
NEAR = 512
FAR = 128
F32 = jnp.float32
BF16 = jnp.bfloat16


def kernel(
    mask_ref, ds_ref, gain_ref, qw_ref, kw_ref, vw_ref, ow_ref, pass_ref, out_ref,
    xs, ws, acc, ow, ds, gain, qw, qpart, qrecv, qsend, qbuf, part, recv, asend, att, osend, orecv,
    loc, pair_s, pair_r, y_s, y_r, ax_s, ax_r, az_s, az_r, bz_s, bz_r, bx_s, bx_r, cy_s, cy_r,
    q2_s, q2_r, q3_s, q3_r, ow_s, ow_r, t1_s, t1_r, t2_s, t2_r,
):
    s = lax.axis_index("section")
    p = lax.axis_index("pb")
    f = lax.axis_index("fsdp")
    z, c = p // 2, lax.rem(p, 2)
    x, y = f // 2, lax.rem(f, 2)

    def zat(k):
        return lax.rem(z + k + NZ, NZ)

    def xat(k):
        return lax.rem(x + k + NX, NX)

    def dev(s_, p_, f_):
        return {"section": s_, "pb": p_, "fsdp": f_}

    partner = dev(s, z * 2 + 1 - c, f)
    ynear = dev(s, p, x * 2 + 1 - y)
    xdev = {k: dev(s, p, xat(k) * 2 + y) for k in (1, -1)}
    zdev = {k: dev(s, zat(k) * 2 + c, f) for k in (1, -1)}
    other_section = dev(1 - s, p, f)

    def rcopy(src, dst, ssem, rsem, to):
        return pltpu.make_async_remote_copy(
            src_ref=src, dst_ref=dst, send_sem=ssem, recv_sem=rsem, device_id=to, device_id_type=MESH
        )

    def half(ref, h):
        return ref.at[:, pl.ds(pl.multiple_of(h * 512, 512), 512)]

    locals_ = [
        pltpu.make_async_copy(ds_ref, ds, loc.at[0]),
        pltpu.make_async_copy(gain_ref, gain, loc.at[1]),
        pltpu.make_async_copy(qw_ref, qw, loc.at[2]),
        pltpu.make_async_copy(half(kw_ref, c), ws.at[z, c, x, y, :, pl.ds(0, 512)], loc.at[3]),
        pltpu.make_async_copy(half(vw_ref, c), ws.at[z, c, x, y, :, pl.ds(512, 512)], loc.at[4]),
        pltpu.make_async_copy(pass_ref, xs.at[c], loc.at[5]),
        pltpu.make_async_copy(ow_ref, ow, loc.at[6]),
    ]
    for copy in locals_:
        copy.start()

    barrier = pltpu.get_barrier_semaphore()

    def greet(to):
        pl.semaphore_signal(barrier, inc=1, device_id=to, device_id_type=MESH)

    def q3_target(i):
        return plane(i), f // 4, z

    def t2_target(k):
        return f * 2 + z // 4, lax.rem(f + k, 8)

    diag = z == f
    for to in (partner, ynear, xdev[1], xdev[-1], zdev[1], zdev[-1], other_section):
        greet(to)
    pl.semaphore_wait(barrier, 7)

    sends = []

    def go(copy):
        copy.start()
        sends.append(copy)

    def pair_copy(i):
        w_ref = (kw_ref, vw_ref)[i]
        return rcopy(
            half(w_ref, 1 - c), ws.at[z, c, x, y, :, pl.ds(512 * i, 512)], pair_s.at[i], pair_r.at[i], partner
        )

    go(pair_copy(0))
    go(pair_copy(1))
    go(rcopy(pass_ref, xs.at[c], pair_s.at[2], pair_r.at[2], partner))

    def land(dst, rsem):
        rcopy(dst, dst, loc.at[7], rsem, partner).wait_recv()

    def plane(i):
        if i == 0:
            return z
        if i == NZ - 1:
            return zat(NZ // 2)
        return zat(-((i + 1) // 2)) if i % 2 else zat(i // 2)

    ys = (y, 1 - y)

    def piece_a(zz, xx, h):
        return ws.at[zz, :, xx, ys[h], :, pl.ds(0, (NEAR, FAR)[h])]

    def piece_b(zz, xx, h):
        return ws.at[zz, :, xx, ys[h], :, pl.ds(NEAR, 1024 - NEAR)]

    def piece_c(zz, h):
        return ws.at[zz, :, :, ys[h], :, pl.ds(FAR, NEAR - FAR)]

    def onward(i, parity):
        if i == NZ - 1:
            return None
        k = (i + 1) // 2
        way = 1 if i % 2 else -1
        if k + 1 < NZ // 2:
            return (i + 2, way)
        if (parity == 0) == (way == 1):
            return (NZ - 1, way)
        return None

    def z_sends(ref, i, col, ssem, rsem):
        nexts = [(1, 1), (2, -1)] if i == 0 else [onward(i, col % 2)]
        for step in nexts:
            if step is not None:
                slot, way = step
                go(rcopy(ref, ref, ssem.at[slot - 1, col], rsem.at[slot - 1, col], zdev[way]))

    xorder = (0, -1, 1, 2)

    def b_go(i, h):
        ref = piece_b(plane(i), x, h)
        for way in (1, -1):
            n = (1 - way) // 2
            go(rcopy(ref, ref, bx_s.at[i, h, n], bx_r.at[i, h, n], xdev[way]))
        z_sends(ref, i, h, bz_s, bz_r)

    def b_z(i):
        for h in range(2):
            land(piece_b(plane(i), x, h), bz_r.at[i - 1, h])
            b_go(i, h)

    def a_z(i):
        for j in range(4):
            for h in range(2):
                ref = piece_a(plane(i), xat(xorder[j]), h)
                land(ref, az_r.at[h, i - 1, j])
                z_sends(ref, i, j, az_s.at[h], az_r.at[h])

    def a_own(h):
        ref = piece_a(z, x, h)
        for way in (1, -1):
            n = (1 - way) // 2
            go(rcopy(ref, ref, ax_s.at[h, n], ax_r.at[h, n], xdev[way]))
        z_sends(ref, 0, 0, az_s.at[h], az_r.at[h])

    def a_x():
        for j in range(1, 4):
            for h in range(2):
                ref = piece_a(z, xat(xorder[j]), h)
                land(ref, ax_r.at[h, j - 1])
                if j == 1:
                    go(rcopy(ref, ref, ax_s.at[h, 2], ax_r.at[h, 2], xdev[1]))
                z_sends(ref, 0, j, az_s.at[h], az_r.at[h])

    def c_go(i):
        ref = piece_c(plane(i), 0)
        go(rcopy(ref, ref, cy_s.at[i], cy_r.at[i], ynear))

    def b_x1(i):
        for h in range(2):
            left, right = piece_b(plane(i), xat(-1), h), piece_b(plane(i), xat(1), h)
            land(left, bx_r.at[i, h, 0])
            land(right, bx_r.at[i, h, 1])
            ref, way = ((left, 1), (right, -1))[h]
            go(rcopy(ref, ref, bx_s.at[i, h, 2], bx_r.at[i, h, 2], xdev[way]))

    def last(i):
        for h in range(2):
            land(piece_b(plane(i), xat(2), h), bx_r.at[i, h, 2])
        land(piece_c(plane(i), 1), cy_r.at[i])

    def project(i):
        zz = plane(i)
        cols = pl.ds(pl.multiple_of(zz * 512, 512), 512)

        def tile(t, carry):
            rows = xs[t // 2, lax.rem(t, 2), :, cols]
            for n in range(4):
                w = ws[zz, :, :, :, :, n * 256 : (n + 1) * 256].reshape(512, 256)
                term = jnp.dot(rows, w, preferred_element_type=F32)
                at = (t, slice(None), slice(n * 256, (n + 1) * 256))
                if i == 0:
                    acc[at] = term
                else:
                    acc[at] += term
            return carry

        lax.fori_loop(0, 4, tile, 0)

    def query_start():
        for copy in locals_[:3]:
            copy.wait()
        wide = ds[...].astype(F32)
        squares = jnp.broadcast_to(jnp.sum(wide * wide, axis=1, keepdims=True), (32, 128))
        scaled = (wide * gain[...].astype(F32).reshape(1, 512)).astype(BF16)
        total = jnp.dot(scaled, qw[...], preferred_element_type=F32)
        for b in range(8):
            qpart[b, :, 0:128] = total[:, b * 128 : (b + 1) * 128]
            qpart[b, :, 128:256] = squares

    def query_reduce():
        for k in range(1, 8):
            to = lax.rem(f + k, 8)
            go(rcopy(qpart.at[to], qrecv.at[k - 1], q2_s.at[k - 1], q2_r.at[k - 1], dev(s, p, to)))

    def query_total():
        total = qpart[f]
        for k in range(7):
            land(qrecv.at[k], q2_r.at[k])
            total = total + qrecv[k]
        scale = lax.rsqrt(total[:, 128:256] / 4096.0 + 1e-06)
        qsend[...] = (total[:, 0:128] * scale).astype(BF16)

    def query_send(i):
        block = lax.rem(f, 4)
        zt, ct, ft = q3_target(i)
        copy = rcopy(qsend, qbuf.at[c, block], q3_s.at[i], q3_r.at[c * 4 + block], dev(s, zt * 2 + ct, ft))
        if i == 0:
            own = diag & (ct == c)

            @pl.when(own)
            def _():
                qbuf[c, block] = qsend[...]

            @pl.when(jnp.logical_not(own))
            def _():
                copy.start()

        else:
            go(copy)

    def query_wait():
        for cs in range(2):
            for b in range(4):
                own = diag & (f // 4 == c) & (cs == c) & (b == lax.rem(f, 4))

                @pl.when(jnp.logical_not(own))
                def _():
                    land(qbuf.at[cs, b], q3_r.at[cs * 4 + b])

        zt, ct, ft = q3_target(0)

        @pl.when(jnp.logical_not(diag & (ct == c)))
        def _():
            rcopy(qsend, qbuf.at[0, 0], q3_s.at[0], q3_r.at[0], partner).wait_send()

    def attend():
        head_of = lax.broadcasted_iota(jnp.int32, (32, 512), 1) // HD
        lane = lax.broadcasted_iota(jnp.int32, (32, 128), 1)
        block_of = lax.broadcasted_iota(jnp.int32, (256, 512), 1) // BLOCK
        for q in range(2):
            query = jnp.concatenate([qbuf[q, b] for b in range(4)], axis=1).astype(F32)
            spread = jnp.concatenate(
                [jnp.where(head_of == h, query, 0.0).astype(BF16) for h in range(8)], axis=0
            )
            keys = jnp.concatenate([acc[q, :, 0:512], acc[2 + q, :, 0:512]], axis=0).astype(BF16)
            values = jnp.concatenate([acc[q, :, 512:1024], acc[2 + q, :, 512:1024]], axis=0).astype(BF16)
            scores = lax.dot_general(spread, keys, (((1,), (1,)), ((), ())), preferred_element_type=F32)
            flags = jnp.zeros((256, 512), jnp.int32)
            for b in range(4):
                flags = jnp.where(block_of == b, mask_ref[f * 2 + q, z * 4 + b], flags)
            shown = flags > 0
            scores = jnp.where(shown, scores, NEGATIVE)
            peak = jnp.max(scores, axis=1, keepdims=True)
            raw = jnp.where(shown, jnp.exp(scores - peak), 0.0)
            totals = jnp.sum(raw, axis=1, keepdims=True)
            wide = jnp.dot(raw.astype(BF16), values, preferred_element_type=F32)
            numer = jnp.zeros((32, 512), F32)
            stats = jnp.zeros((32, 128), F32)
            for h in range(8):
                rows = slice(h * 32, (h + 1) * 32)
                numer = jnp.where(head_of == h, wide[rows], numer)
                stats = jnp.where(lane == h, peak[rows], stats)
                stats = jnp.where(lane == h + 64, totals[rows], stats)
            for ah in range(2):
                rows = slice(ah * 16, (ah + 1) * 16)
                for ch in range(2):
                    rank = (q * 2 + ah) * 2 + ch
                    part[rank, :, 0:256] = numer[rows, ch * 256 : (ch + 1) * 256]
                    part[rank, :, 256:384] = stats[rows]

    def combine_send():
        for k in range(1, 8):
            zt = zat(k)
            go(rcopy(part.at[zt], recv.at[k - 1], t1_s.at[k - 1], t1_r.at[k - 1], dev(s, zt * 2 + c, f)))

    def combine():
        pieces = [part[z]]
        for k in range(7):
            land(recv.at[k], t1_r.at[k])
            pieces.append(recv[k])
        top = pieces[0][:, 256:384]
        for piece in pieces[1:]:
            top = jnp.maximum(top, piece[:, 256:384])
        col_head = lax.broadcasted_iota(jnp.int32, (16, 256), 1) // HD
        first = lax.rem(z, 2) == 0

        def widen(stat, base):
            low = jnp.zeros((16, 256), F32)
            for h in range(4):
                one = jnp.where(first, stat[:, base + h : base + h + 1], stat[:, base + h + 4 : base + h + 5])
                low = jnp.where(col_head == h, one, low)
            return low

        top_wide = widen(top, 0)
        numer = jnp.zeros((16, 256), F32)
        total = jnp.zeros((16, 256), F32)
        for piece in pieces:
            stat = piece[:, 256:384]
            factor = jnp.exp(widen(stat, 0) - top_wide)
            numer = numer + piece[:, 0:256] * factor
            total = total + widen(stat, 64) * factor
        asend[...] = (numer / total).astype(BF16)

    def spot():
        return c, lax.rem(z, 2), lax.rem(z // 2, 2)

    def scatter():
        b, d, e = spot()
        sem = t2_r.at[(b * 2 + d) * 2 + e]
        for k in range(8):
            pt, ft = t2_target(k)
            copy = rcopy(asend, att.at[b, d, e], t2_s.at[k], sem, dev(s, pt, ft))
            if k == 0:
                own = pt == p

                @pl.when(own)
                def _():
                    att[b, d, e] = asend[...]

                @pl.when(jnp.logical_not(own))
                def _():
                    copy.start()

            else:
                go(copy)

    def finish():
        locals_[6].wait()
        b, d, e = spot()
        own_code = (b * 2 + d) * 2 + e
        pt, ft = t2_target(0)
        own = pt == p
        total = jnp.zeros((32, 512), F32)
        for ci in range(2):
            for ch in range(2):
                halves = []
                for ah in range(2):
                    code = (ci * 2 + ch) * 2 + ah

                    @pl.when(jnp.logical_not(own & (own_code == code)))
                    def _():
                        land(att.at[ci, ch, ah], t2_r.at[code])

                    halves.append(att[ci, ch, ah])
                rows = jnp.concatenate(halves, axis=0)
                at = ci * 512 + ch * 256
                total = total + jnp.dot(rows, ow[at : at + 256, :], preferred_element_type=F32)
        osend[...] = total.astype(BF16)
        go(rcopy(osend, orecv, ow_s.at[0], ow_r.at[0], other_section))
        land(orecv, ow_r.at[0])
        out_ref[...] = (osend[...].astype(F32) + orecv[...].astype(F32)).astype(BF16)

        @pl.when(jnp.logical_not(own))
        def _():
            rcopy(asend, att.at[0, 0, 0], t2_s.at[0], t2_r.at[0], partner).wait_send()

    locals_[3].wait()
    locals_[4].wait()
    land(ws.at[z, 1 - c, x, y, :, pl.ds(0, 512)], pair_r.at[0])
    land(ws.at[z, 1 - c, x, y, :, pl.ds(512, 512)], pair_r.at[1])
    own_b, own_c = piece_b(z, x, 0), ws.at[z, :, x, y, :, pl.ds(0, FAR)]
    go(rcopy(own_b, own_b, y_s.at[0], y_r.at[0], ynear))
    go(rcopy(own_c, own_c, y_s.at[1], y_r.at[1], ynear))
    b_go(0, 0)
    a_own(0)
    query_start()
    land(piece_b(z, x, 1), y_r.at[0])
    b_go(0, 1)
    land(piece_a(z, x, 1), y_r.at[1])
    a_own(1)
    a_x()
    c_go(0)
    query_reduce()
    for t in range(1, NZ + 2):
        if t < NZ:
            b_z(t)
            a_z(t)
            c_go(t)
        if t <= NZ:
            b_x1(t - 1)
        if t == 2:
            query_total()
            query_send(0)
            query_send(1)
            locals_[5].wait()
            land(xs.at[1 - c], pair_r.at[2])
        if 2 <= t < NZ:
            query_send(t)
        if t >= 2:
            last(t - 2)
            project(t - 2)
    query_wait()
    attend()
    combine_send()
    combine()
    scatter()
    finish()
    for copy in sends:
        copy.wait_send()


def shards(
    decoder_states, norm_gain, query_weight, key_weight, value_weight, out_weight, passage_states, block_mask
):
    anywhere = pl.BlockSpec(memory_space=pl.ANY)
    dma = pltpu.SemaphoreType.DMA
    out = pl.pallas_call(
        kernel,
        out_shape=jax.ShapeDtypeStruct((32, 512), BF16),
        in_specs=[pl.BlockSpec(memory_space=pltpu.SMEM)] + [anywhere] * 7,
        out_specs=pl.BlockSpec(memory_space=pltpu.VMEM),
        scratch_shapes=[
            pltpu.VMEM((2, 2, 256, 4096), BF16),
            pltpu.VMEM((NZ, 2, NX, 2, 32, 1024), BF16),
            pltpu.VMEM((4, 256, 1024), F32),
            pltpu.VMEM((1024, 512), BF16),
            pltpu.VMEM((32, 512), BF16),
            pltpu.VMEM((512,), BF16),
            pltpu.VMEM((512, 1024), BF16),
            pltpu.VMEM((8, 32, 256), F32),
            pltpu.VMEM((7, 32, 256), F32),
            pltpu.VMEM((32, 128), BF16),
            pltpu.VMEM((2, 4, 32, 128), BF16),
            pltpu.VMEM((8, 16, 384), F32),
            pltpu.VMEM((7, 16, 384), F32),
            pltpu.VMEM((16, 256), BF16),
            pltpu.VMEM((2, 2, 2, 16, 256), BF16),
            pltpu.VMEM((32, 512), BF16),
            pltpu.VMEM((32, 512), BF16),
            dma((8,)),
            dma((3,)), dma((3,)),
            dma((2,)), dma((2,)),
            dma((2, 3)), dma((2, 3)),
            dma((2, NZ - 1, 4)), dma((2, NZ - 1, 4)),
            dma((NZ - 1, 2)), dma((NZ - 1, 2)),
            dma((NZ, 2, 3)), dma((NZ, 2, 3)),
            dma((NZ,)), dma((NZ,)),
            dma((7,)), dma((7,)),
            dma((8,)), dma((8,)),
            dma((1,)), dma((1,)),
            dma((7,)), dma((7,)),
            dma((8,)), dma((8,)),
        ],
        compiler_params=pltpu.CompilerParams(
            collective_id=0, has_side_effects=True, vmem_limit_bytes=56 * 1024 * 1024
        ),
        name="reader",
    )(
        block_mask, decoder_states[0], norm_gain, query_weight, key_weight, value_weight,
        out_weight, passage_states,
    )
    return out[None]


def solution(mesh):
    placed = (
        P("pb", None, "fsdp"),
        P("fsdp"),
        P("fsdp", "section"),
        P(("pb", "fsdp"), "section"),
        P(("pb", "fsdp"), "section"),
        P("section", "fsdp"),
        P("fsdp", "pb", None),
        P(),
    )
    return jax.shard_map(
        shards, mesh=mesh, in_specs=placed, out_specs=P("pb", None, "fsdp"), check_vma=False
    )
```

time: 101 us -> 84.6 us (0.84)
  Pallas kernels: 98 us -> 83 us
  local copies, waits for them, and re-layouts: 2.63 us -> 1.38 us
    pallas_call x1, Pallas kernels: 98 us -> 83 us  [shards(): pl.pallas_call(kernel, out_shape=jax.ShapeDtypeStruct((32, 512), BF16), i...]
    broadcast_in_dim x1 -> x0, local copies, waits for them, and re-layouts: 1.26 us -> none  [shards(): norm_gain[None]]
where the time goes in v2:
time: 84.6 us; the launch traced here: 84.4 us
  Pallas kernels  83 us (98%)
  local copies, waits for them, and re-layouts  1.38 us (2%)
    pallas_call x1, Pallas kernels, shards(): pl.pallas_call(kernel, out_shape=jax.ShapeDtypeStruct((32, 512), BF16), i...  83 us

profile of v2, /device:TPU:1, one launch (start us, length us, event | category | flops | bytes accessed | tf_op | source)
XLA Modules:
  0.0 84.4 jit_solution(4535609450906945114)
XLA Ops:
  0.0 83.0 %reader.1 = bf16[32,512]{1,0:T(8,128)(2,1)} custom-call(s32[16,32]{1,0:T(8,128)} %mask_ref.1, bf16[32,512]{1,0:T(8,128)(2,1)} %bitcast.3, bf16[512]{0:T(512)(128)(2,1)} %gain_ref.1, bf16[512,1024]{1,0:T(8,128)(2,1)} %qw_ref.1, bf16[32,1024]{1,0:T(8,128)(2,1)} %kw_ref.1, bf16[32,1024]{1,0:T(8,128)(2,1)} %vw_ref.1, bf16[1024,512]{1,0:T(8,128)(2,1)} %ow_ref.1, ...), custom_call_target="tpu_custom_call" | custom-call | tf_op jit(solution)/shard_map/reader/pallas_call | solution.py:438
  83.0 1.4 %copy.10 = bf16[1,32,512]{2,1,0:T(8,128)(2,1)} copy(bf16[1,32,512]{2,1,0:T(8,128)(2,1)} %bitcast.2) | data formatting | bytes 65536
